TPU v7x, 32 devices: a whole 2x2x4 slice. The times are simulated.
32 devices in a mesh: ta: 16 (over z, y, x), gz: 2 (over core).
Axes of the slice: x: 2, y: 2, z: 4, core: 2. Of those that a mesh axis runs over, the one named last changes fastest.
Arguments:
- time_links: float32 [2, 3, 3, 32, 8, 256], P(None, None, None, 'ta', 'gz'), may hold values from -1 to 1, as said below
- space_links: float32 [3, 2, 3, 3, 32, 8, 256], P(None, None, None, None, 'ta', 'gz'), may hold values from -1 to 1, as said below
Outputs:
- gauge: float32 [2, 3, 3, 32, 8, 256], P(None, None, None, 'ta', 'gz')
- links_fixed: float32 [3, 2, 3, 3, 32, 8, 256], P(None, None, None, None, 'ta', 'gz')
- action_profile: float32 [32, 8], P('ta', 'gz')
- action_mean: float32 [], replicated
Inputs may be any that keep to these rules, and one draw needn't show every extreme that they name: `time_links`: every 3 x 3 complex matrix is unitary up to float32 rounding. `space_links`: every 3 x 3 complex matrix is unitary up to float32 rounding.
All inputs are finite; a program needn't handle non-finite values.
Results may differ from a plain program's by a relative error of at most 0.00024.
Values sent between devices are 32-bit elements; how exact they have to be, the bound alone decides.
A program may use at most 64 MiB of HBM per device.

v0:
```python
import jax
import jax.numpy as jnp
from jax import lax
from jax.sharding import PartitionSpec as P

X = 16
Y = 16


def entering(shard, axis, combine, identity):
    length, mine = (lax.axis_size(axis), lax.axis_index(axis))
    everything = lax.all_gather(shard, axis)
    start = jnp.broadcast_to(jnp.asarray(identity, shard.dtype), shard.shape)

    def hop(k, before):
        reached = k < mine
        new = combine(before, everything[k])
        return jnp.where(reached, new, before)

    return lax.fori_loop(0, length, hop, start)


def from_behind(block, axis, distance):
    devices = range(lax.axis_size(axis))
    route = [((i - distance) % len(devices), i) for i in devices]
    return lax.ppermute(block, axis, route)


def complex_product(first_pair, second_pair):
    first_real, first_imag = first_pair
    second_real, second_imag = second_pair
    real_part = jnp.sum(
        first_real[:, :, None] * second_real[None] - first_imag[:, :, None] * second_imag[None],
        axis=1,
    )
    imag_part = jnp.sum(
        first_real[:, :, None] * second_imag[None] + first_imag[:, :, None] * second_real[None],
        axis=1,
    )
    return (real_part, imag_part)


def dagger(matrix_pair):
    return (jnp.swapaxes(matrix_pair[0], 0, 1), -jnp.swapaxes(matrix_pair[1], 0, 1))


def plane_step(matrix_pair, direction):

    def shifted(values):
        leading = values.shape[:-1]
        lattice_grid = values.reshape(leading + (X, Y))
        lattice_grid = jnp.roll(lattice_grid, -1, axis=lattice_grid.ndim - 2 + direction)
        return lattice_grid.reshape(leading + (X * Y,))

    return (shifted(matrix_pair[0]), shifted(matrix_pair[1]))


def upward_z(matrix_pair, upper_layer):
    return (
        jnp.concatenate([matrix_pair[0][..., 1:, :], upper_layer[0]], axis=-2),
        jnp.concatenate([matrix_pair[1][..., 1:, :], upper_layer[1]], axis=-2),
    )


def plaquette_density(link_set, forward_x, forward_y):
    forward_z = [forward_x, forward_y]
    terms = []
    for first_dir, second_dir in ((0, 1), (0, 2), (1, 2)):
        along_first = link_set[first_dir]
        along_second = link_set[second_dir]
        second_moved = plane_step(along_second, first_dir)
        if second_dir < 2:
            first_moved = plane_step(along_first, second_dir)
        else:
            first_moved = forward_z[first_dir]
        loop_matrix = complex_product(
            complex_product(along_first, second_moved),
            complex_product(dagger(first_moved), dagger(along_second)),
        )
        trace_real = loop_matrix[0][0, 0] + loop_matrix[0][1, 1] + loop_matrix[0][2, 2]
        terms.append(1.0 - trace_real / 3.0)
    return terms[0] + terms[1] + terms[2]


def on_device(time_links, space_links):
    local_steps = time_links.shape[3]
    layer_count = time_links.shape[4]
    site_count = time_links.shape[5]
    unit_matrix = jnp.eye(3, dtype=jnp.float32)[:, :, None, None]
    unit_real = jnp.broadcast_to(unit_matrix, (3, 3, layer_count, site_count))
    running = (unit_real, jnp.zeros_like(unit_real))
    prefixes = []
    for step_index in range(local_steps):
        prefixes.append(running)
        running = complex_product(
            running, (time_links[0, :, :, step_index], time_links[1, :, :, step_index])
        )

    def combine(earlier, later):
        return jnp.stack(complex_product((earlier[0], earlier[1]), (later[0], later[1])))

    identity_pair = jnp.stack([unit_real, jnp.zeros_like(unit_real)])
    carried = entering(jnp.stack(running), "ta", combine, identity_pair)
    carried_pair = (carried[0], carried[1])
    time_slices = [complex_product(carried_pair, prefix_pair) for prefix_pair in prefixes]
    gauge_pair = (
        jnp.stack([piece[0] for piece in time_slices], axis=2),
        jnp.stack([piece[1] for piece in time_slices], axis=2),
    )
    first_layer = jnp.stack([gauge_pair[0][..., 0:1, :], gauge_pair[1][..., 0:1, :]])
    gauge_above = from_behind(first_layer, "gz", -1)
    gauge_next_z = upward_z(gauge_pair, (gauge_above[0], gauge_above[1]))
    fixed = []
    for direction in range(3):
        link_pair = (space_links[direction, 0], space_links[direction, 1])
        ahead = plane_step(gauge_pair, direction) if direction < 2 else gauge_next_z
        fixed.append(complex_product(complex_product(gauge_pair, link_pair), dagger(ahead)))
    links_fixed = jnp.stack([jnp.stack(pair) for pair in fixed])
    layers_above = from_behind(space_links[0:2, ..., 0:1, :], "gz", -1)
    link_set = [(space_links[direction, 0], space_links[direction, 1]) for direction in range(3)]
    forward_x = upward_z(link_set[0], (layers_above[0, 0], layers_above[0, 1]))
    forward_y = upward_z(link_set[1], (layers_above[1, 0], layers_above[1, 1]))
    density = plaquette_density(link_set, forward_x, forward_y)
    action_profile = jnp.mean(density, axis=-1) / 3.0
    local_total = jnp.sum(action_profile)
    whole_total = lax.psum(local_total, ("ta", "gz"))
    action_mean = whole_total / (action_profile.size * lax.axis_size("ta") * lax.axis_size("gz"))
    return (jnp.stack(gauge_pair), links_fixed, action_profile, action_mean)


def solution(mesh):
    return jax.shard_map(
        on_device,
        mesh=mesh,
        in_specs=(
            P(None, None, None, "ta", "gz", None),
            P(None, None, None, None, "ta", "gz", None),
        ),
        out_specs=(
            P(None, None, None, "ta", "gz", None),
            P(None, None, None, None, "ta", "gz", None),
            P("ta", "gz"),
            P(),
        ),
        check_vma=False,
    )
```

profile of v0, /device:TPU:0, one launch (start us, length us, event | category | flops | bytes accessed | tf_op | source)
XLA Modules:
  0.0 148.0 jit_solution(17676963432240633824)
XLA Ops:
  7.2 0.9 slice_bitcast_fusion.5
  8.1 0.8 broadcast_multiply_fusion.2
  9.8 0.7 pad_maximum_fusion.13
  10.5 0.7 slice.262
  11.6 0.9 fusion.19
  12.8 0.9 slice.309
  14.5 0.9 slice.311
  17.4 1.1 reshape_squeeze.21
  18.5 0.9 slice.300
  20.0 2.1 %pad_maximum_fusion.5 = f32[3,3,2,4,16,16]{5,4,3,2,1,0:T(8,128)} fusion(f32[3,3,2,4,1,16]{5,4,3,2,1,0:T(1,128)} %slice.310, f32[3,3,2,4,15,16]{5,4,3,2,1,0:T(8,128)} %slice.309), kind=kLoop, calls=%fused_computation.15 | loop fusion | flops 18432 | bytes 147456 | tf_op jit(solution)/shard_map/jit(_roll_static)/concatenate | solution.py:52
  22.1 2.0 %mul.986 = f32[3,3,2,4,256]{4,3,2,1,0:T(4,128)} reshape(f32[3,3,2,4,16,16]{5,4,3,2,1,0:T(8,128)} %pad_maximum_fusion.5) | data formatting | bytes 147456 | tf_op jit(solution)/shard_map/mul | solution.py:33
  24.1 1.7 %pad_maximum_fusion.6 = f32[3,3,2,4,16,16]{5,4,3,2,1,0:T(8,128)} fusion(f32[3,3,2,4,1,16]{5,4,3,2,1,0:T(1,128)} %slice.312, f32[3,3,2,4,15,16]{5,4,3,2,1,0:T(8,128)S(1)} %copy-done.2), kind=kLoop, calls=%fused_computation.16 | loop fusion | flops 18432 | bytes 147456 | tf_op jit(solution)/shard_map/jit(_roll_static)/concatenate | solution.py:52
  25.8 2.0 %mul.989 = f32[3,3,2,4,256]{4,3,2,1,0:T(4,128)} reshape(f32[3,3,2,4,16,16]{5,4,3,2,1,0:T(8,128)} %pad_maximum_fusion.6) | data formatting | bytes 147456 | tf_op jit(solution)/shard_map/mul | solution.py:33
  28.0 0.9 mul.1009
  29.1 0.9 mul.1013
  30.1 0.9 mul.499
  31.2 0.9 mul.503
  34.7 1.0 negate_bitcast_fusion.1
  35.7 0.8 subtract_reduce_fusion.8
  36.5 0.8 slice_bitcast_fusion.9
  37.4 1.3 subtract_reduce_fusion.5
  38.7 31.3 %all-gather.3.cloned.1.call-done = f32[32,3,3,4,256]{4,3,2,1,0:T(4,128)} async-done(((f32[2,3,3,4,256]{4,3,2,1,0:T(4,128)}), f32[32,3,3,4,256]{4,3,2,1,0:T(4,128)}) %all-gather.3.cloned.1.call-update) | async-done | bytes 1179664 | tf_op jit(solution)/shard_map/all_gather | solution.py:12
  70.0 15.6 %while.13 = (s32[]{:T(128)}, f32[2,3,3,4,256]{4,3,2,1,0:T(4,128)S(1)}, s32[]{:T(128)}, f32[16,2,3,3,4,256]{5,4,3,2,1,0:T(4,128)}, s32[]{:T(128)}, /*index=5*/s32[]{:T(128)}, s32[]{}) while((s32[]{:T(128)}, f32[2,3,3,4,256]{4,3,2,1,0:T(4,128)S(1)}, s32[]{:T(128)}, f32[16,2,3,3,4,256]{5,4,3,2,1,0:T(4,128)}, s32[]{:T(128)}, /*index=5*/s32[]{:T(128)}, ...), condition=%wide.region_7.8_spmd, body=%wide.region_4.7_spmd.sunk | while | flops 239620 | bytes 737387 | solution.py:20
  70.0 0.8 dynamic-slice_bitcast_fusion.3
  71.0 0.8 dynamic-slice_bitcast_fusion.3
  72.0 0.8 dynamic-slice_bitcast_fusion.3
  73.0 0.8 dynamic-slice_bitcast_fusion.3
  74.0 0.8 dynamic-slice_bitcast_fusion.3
  74.9 0.8 dynamic-slice_bitcast_fusion.3
  75.9 0.8 dynamic-slice_bitcast_fusion.3
  76.9 0.8 dynamic-slice_bitcast_fusion.3
  77.9 0.8 dynamic-slice_bitcast_fusion.3
  78.8 0.8 dynamic-slice_bitcast_fusion.3
  79.8 0.8 dynamic-slice_bitcast_fusion.3
  80.8 0.8 dynamic-slice_bitcast_fusion.3
  81.8 0.8 dynamic-slice_bitcast_fusion.3
  82.7 0.8 dynamic-slice_bitcast_fusion.3
  83.7 0.8 dynamic-slice_bitcast_fusion.3
  84.7 0.8 dynamic-slice_bitcast_fusion.3
  87.8 0.9 slice.280
  89.3 0.7 pad_maximum_fusion.12
  90.6 0.7 fusion.20
  91.9 0.6 fusion
  94.4 1.1 subtract_reduce_fusion.9
  96.1 1.2 fusion.18
  98.8 38.6 %psum.7 = f32[]{:T(128)} all-reduce(f32[]{:T(128)} %get-tuple-element.158), channel_id=1, replica_groups=mesh['ta'=16,'gz'=2] {'ta','gz'}, use_global_device_ids=true, to_apply=%region_41.42 | all-reduce | flops 1 | bytes 8 | tf_op jit(solution)/shard_map/psum | solution.py:126
  137.4 0.7 copy.176
  139.1 0.9 pad_maximum_fusion.9
  (233 shorter events, 18.9 us)
Async XLA Ops:
  7.2 3.3 %copy-start.11 = (f32[3,2,3,3,2,4,256]{6,5,4,3,2,1,0:T(4,128)S(1)}, f32[3,2,3,3,2,4,256]{6,5,4,3,2,1,0:T(4,128)}, u32[]{:S(2)}) copy-start(f32[3,2,3,3,2,4,256]{6,5,4,3,2,1,0:T(4,128)} %param.5) | copy-start | bytes 1327108
  7.2 62.9 %all-gather.3.cloned.1.call-start = ((), (), s32[]{:S(2)}) async-start(), calls=%async_computation | async-start | bytes 1253376 | tf_op jit(solution)/shard_map/all_gather | solution.py:12
  11.1 25.4 %collective-permute-start.1 = (f32[2,2,3,3,2,1,256]{6,5,4,3,2,1,0:T(1,128)}, f32[2,2,3,3,2,1,256]{6,5,4,3,2,1,0:T(1,128)}, u32[]{:S(2)}, u32[]{:S(2)}) collective-permute-start(f32[2,2,3,3,2,1,256]{6,5,4,3,2,1,0:T(1,128)} %slice.262), channel_id=1, source_target_pairs={{1,0},{0,1},{3,2},{2,3},{5,4},{4,5},{7,6},{6,7},{9,8},{8,9},{11,10... | collective-permute-start | bytes 221192 | tf_op jit(solution)/shard_map/ppermute | solution.py:26
  20.0 4.0 %copy-start.2 = (f32[3,3,2,4,15,16]{5,4,3,2,1,0:T(8,128)S(1)}, f32[3,3,2,4,15,16]{5,4,3,2,1,0:T(8,128)}, u32[]{:S(2)}) copy-start(f32[3,3,2,4,15,16]{5,4,3,2,1,0:T(8,128)} %slice.311) | copy-start | bytes 207364
  28.9 1.2 copy-start.45
  29.1 2.0 %copy-start.1 = (f32[3,3,2,4,15,16]{5,4,3,2,1,0:T(8,128)S(1)}, f32[3,3,2,4,15,16]{5,4,3,2,1,0:T(8,128)}, u32[]{:S(2)}) copy-start(f32[3,3,2,4,15,16]{5,4,3,2,1,0:T(8,128)} %slice.300) | copy-start | bytes 207364
  29.1 2.0 %copy-start.46 = (f32[3,3,2,4,1,16]{5,4,3,2,1,0:T(1,128)S(1)}, f32[3,3,2,4,1,16]{5,4,3,2,1,0:T(1,128)}, u32[]{:S(2)}) copy-start(f32[3,3,2,4,1,16]{5,4,3,2,1,0:T(1,128)} %slice.301) | copy-start | bytes 13828
  30.1 2.0 %copy-start.9 = (f32[3,3,2,4,256]{4,3,2,1,0:T(4,128)S(1)}, f32[3,3,2,4,256]{4,3,2,1,0:T(4,128)}, u32[]{:S(2)}) copy-start(f32[3,3,2,4,256]{4,3,2,1,0:T(4,128)} %get-tuple-element.172) | copy-start | bytes 221188
  31.1 1.1 copy-start.5
  31.1 1.1 copy-start.7
  31.1 1.2 copy-start.3
  31.1 1.2 copy-start.39
  32.7 0.9 copy-start.38
  34.1 1.6 %copy-start.29 = (f32[3,3,2,4,256]{4,3,2,0,1:T(4,128)S(1)}, f32[3,3,2,4,256]{4,3,2,0,1:T(4,128)}, u32[]{:S(2)}) copy-start(f32[3,3,2,4,256]{4,3,2,0,1:T(4,128)} %get-tuple-element.166) | copy-start | bytes 221188
  34.3 3.1 %copy-start.26 = (f32[3,3,2,4,256]{4,3,2,0,1:T(4,128)S(1)}, f32[3,3,2,4,256]{4,3,2,0,1:T(4,128)}, u32[]{:S(2)}) copy-start(f32[3,3,2,4,256]{4,3,2,0,1:T(4,128)} %get-tuple-element.169) | copy-start | bytes 221188
  70.0 15.7 %copy-start.17 = (f32[3,3,4,256]{3,2,1,0:T(4,128)S(1)}, f32[3,3,4,256]{3,2,1,0:T(4,128)}, u32[]{:S(2)}) copy-start(f32[3,3,4,256]{3,2,1,0:T(4,128)} %copy-done.16) | copy-start | bytes 110596
  70.0 15.7 %copy-start.19 = (f32[3,3,4,256]{3,2,1,0:T(4,128)S(1)}, f32[3,3,4,256]{3,2,1,0:T(4,128)}, u32[]{:S(2)}) copy-start(f32[3,3,4,256]{3,2,1,0:T(4,128)} %copy-done.18) | copy-start | bytes 110596
  85.9 5.3 %copy-start.12 = (f32[3,3,4,256]{3,2,1,0:T(4,128)}, f32[3,3,4,256]{3,2,1,0:T(4,128)S(1)}, u32[]{:S(2)}) copy-start(f32[3,3,4,256]{3,2,1,0:T(4,128)S(1)} %get-tuple-element.142) | copy-start | bytes 110596
  85.9 5.3 %copy-start.14 = (f32[3,3,4,256]{3,2,1,0:T(4,128)}, f32[3,3,4,256]{3,2,1,0:T(4,128)S(1)}, u32[]{:S(2)}) copy-start(f32[3,3,4,256]{3,2,1,0:T(4,128)S(1)} %get-tuple-element.146) | copy-start | bytes 110596
  93.0 0.9 copy-start.4
  93.1 0.9 copy-start.6
  93.1 0.9 copy-start.8
  93.1 1.0 copy-start.10
  93.1 1.0 copy-start.20
  93.1 1.0 copy-start.21
  93.1 1.1 copy-start.30
  93.1 1.1 copy-start.31
  93.1 1.1 copy-start.32
  93.1 1.1 copy-start.33
  93.2 1.1 copy-start.34
  93.2 1.2 copy-start.35
  93.2 1.2 copy-start.36
  93.2 1.2 copy-start.37
  93.7 1.8 %copy-start.22 = (f32[3,3,2,4,256]{4,3,2,1,0:T(4,128)S(1)}, f32[3,3,2,4,256]{4,3,2,1,0:T(4,128)}, u32[]{:S(2)}) copy-start(f32[3,3,2,4,256]{4,3,2,1,0:T(4,128)} %get-tuple-element.112) | copy-start | bytes 221188
  93.7 1.8 %copy-start.23 = (f32[3,3,2,4,256]{4,3,2,1,0:T(4,128)S(1)}, f32[3,3,2,4,256]{4,3,2,1,0:T(4,128)}, u32[]{:S(2)}) copy-start(f32[3,3,2,4,256]{4,3,2,1,0:T(4,128)} %get-tuple-element.113) | copy-start | bytes 221188
  93.7 1.8 %copy-start.24 = (f32[3,3,2,4,256]{4,3,2,1,0:T(4,128)S(1)}, f32[3,3,2,4,256]{4,3,2,1,0:T(4,128)}, u32[]{:S(2)}) copy-start(f32[3,3,2,4,256]{4,3,2,1,0:T(4,128)} %get-tuple-element.140) | copy-start | bytes 221188
  93.7 1.8 %copy-start.25 = (f32[3,3,2,4,256]{4,3,2,1,0:T(4,128)S(1)}, f32[3,3,2,4,256]{4,3,2,1,0:T(4,128)}, u32[]{:S(2)}) copy-start(f32[3,3,2,4,256]{4,3,2,1,0:T(4,128)} %get-tuple-element.141) | copy-start | bytes 221188
  94.4 1.3 copy-start.27
  94.4 1.3 copy-start.28
  95.5 1.8 %copy-start.43 = (f32[3,3,2,4,1,16]{5,4,3,1,0,2:T(1,128)S(1)}, f32[3,3,2,4,1,16]{5,4,3,1,0,2:T(1,128)}, u32[]{:S(2)}) copy-start(f32[3,3,2,4,1,16]{5,4,3,1,0,2:T(1,128)} %slice.283) | copy-start | bytes 13828
  96.0 1.7 %copy-start = (f32[3,3,2,4,15,16]{5,4,3,1,0,2:T(8,128)S(1)}, f32[3,3,2,4,15,16]{5,4,3,1,0,2:T(8,128)}, u32[]{:S(2)}) copy-start(f32[3,3,2,4,15,16]{5,4,3,1,0,2:T(8,128)} %slice.280) | copy-start | bytes 207364
  96.0 1.7 %copy-start.44 = (f32[3,3,2,4,1,16]{5,4,3,1,0,2:T(1,128)S(1)}, f32[3,3,2,4,1,16]{5,4,3,1,0,2:T(1,128)}, u32[]{:S(2)}) copy-start(f32[3,3,2,4,1,16]{5,4,3,1,0,2:T(1,128)} %slice.281) | copy-start | bytes 13828
  97.8 0.9 copy-start.40
  97.8 0.9 copy-start.41
  97.8 0.9 copy-start.13
  97.9 0.9 copy-start.15
  98.2 40.6 %copy-start.42 = (f32[3,3,2,3,256]{4,3,1,0,2:T(4,128)S(1)}, f32[3,3,2,3,256]{4,3,1,0,2:T(4,128)}, u32[]{:S(2)}) copy-start(f32[3,3,2,3,256]{4,3,1,0,2:T(4,128)} %fusion) | copy-start | bytes 165892
  98.2 40.5 %collective-permute-start = (f32[2,3,3,2,1,256]{5,3,2,1,4,0:T(2,128)S(1)}, f32[2,3,3,2,1,256]{5,3,2,1,4,0:T(2,128)S(1)}, u32[]{:S(2)}, u32[]{:S(2)}) collective-permute-start(f32[2,3,3,2,1,256]{5,3,2,1,4,0:T(2,128)S(1)} %pad_maximum_fusion.14), channel_id=1, source_target_pairs={{1,0},{0,1},{3,2},{2,3},{5,4},{4,5},{7,6},{6,7},{9,8},{8,9},{11,10... | collective-permute-start | bytes 110600 | tf_op jit(solution)/shard_map/ppermute | solution.py:26
  (4 other events, 2.8 us)
Sparse Core Ops, SparseCore 0:
  11.4 58.6 all-gather.2
where the time goes:
time: 150 us; the launch traced here: 148 us
  local copies, waits for them, and re-layouts  39.8 us (27%)
  blocking collectives  38.6 us (26%)
  waiting for transfers between devices  31.3 us (21%)
  other arithmetic  20.7 us (14%)
  between operations  16.8 us (11%)
    psum x1, blocking collectives, on_device(): whole_total = lax.psum(local_total, ('ta', 'gz'))  38.6 us
    all_gather x1, waiting for transfers between devices, entering(): everything = lax.all_gather(shard, axis)  31.3 us
    mul x37, local copies, waits for them, and re-layouts, complex_product(): first_real[:, :, None] * second_real[None]  17.5 us
    slice x18, local copies, waits for them, and re-layouts, shifted(): jnp.roll(lattice_grid, -1, axis=lattice_grid.ndim - 2 + direction)  8.75 us
    reduce_sum x26, other arithmetic, complex_product(): jnp.sum(first_real[:, :, None] * second_real[None] - first_imag[:, :, Non...  5.87 us
    concatenate x9, other arithmetic, shifted(): jnp.roll(lattice_grid, -1, axis=lattice_grid.ndim - 2 + direction)  4.93 us
    mul x3, local copies, waits for them, and re-layouts, complex_product(): first_imag[:, :, None] * second_imag[None]  3.78 us
  transfers between devices with their start and end apart: 3, of which 1 were waited for; matrix products, arithmetic and copies ran while one was open for 19% of the time, Pallas kernels for 0%

commit v1 on v0

v1 whole, which is shorter than its diff:
```python
import functools

import jax
import jax.numpy as jnp
from jax import lax
from jax.experimental import pallas as pl
from jax.experimental.pallas import tpu as pltpu
from jax.sharding import PartitionSpec as P

X = 16
Y = 16
LANES = 128
MESH = pl.DeviceIdType.MESH
PACK = 16


def to_rows(a):
    lead, (z, s), n = a.shape[:-2], a.shape[-2:], a.ndim - 2
    a = jnp.swapaxes(a.reshape(lead + (z, s // LANES, LANES)), n, n + 1)
    return a.reshape(lead + (z * (s // LANES), LANES))


def from_rows(a, z, s):
    lead, n = a.shape[:-2], a.ndim - 2
    a = jnp.swapaxes(a.reshape(lead + (s // LANES, z, LANES)), n, n + 1)
    return a.reshape(lead + (z, s))


def product(a, b, rows=(0, 1, 2)):
    re, im = {}, {}
    for i in rows:
        for j in range(3):
            r = m = None
            for k in range(3):
                rr = a[0][i, k] * b[0][k, j] - a[1][i, k] * b[1][k, j]
                mm = a[0][i, k] * b[1][k, j] + a[1][i, k] * b[0][k, j]
                r = rr if r is None else r + rr
                m = mm if m is None else m + mm
            re[i, j], im[i, j] = r, m
    return re, im


def product_dagger(a, b):
    re, im = {}, {}
    for i in range(3):
        for j in range(3):
            r = m = None
            for k in range(3):
                rr = a[0][i, k] * b[0][j, k] + a[1][i, k] * b[1][j, k]
                mm = a[1][i, k] * b[0][j, k] - a[0][i, k] * b[1][j, k]
                r = rr if r is None else r + rr
                m = mm if m is None else m + mm
            re[i, j], im[i, j] = r, m
    return re, im


def cross_conj(m):
    re, im = m
    out_re, out_im = [], []
    for j in range(3):
        p, q = (j + 1) % 3, (j + 2) % 3
        out_re.append(
            (re[0, p] * re[1, q] - im[0, p] * im[1, q])
            - (re[0, q] * re[1, p] - im[0, q] * im[1, p])
        )
        out_im.append(
            (re[0, q] * im[1, p] + im[0, q] * re[1, p])
            - (re[0, p] * im[1, q] + im[0, p] * re[1, q])
        )
    return out_re, out_im


def determinant(m):
    wr, wi = cross_conj(m)
    re, im = m
    dr = sum(wr[j] * re[2, j] + wi[j] * im[2, j] for j in range(3))
    di = sum(wr[j] * im[2, j] - wi[j] * re[2, j] for j in range(3))
    return dr, di


def with_last_row(top, det):
    wr, wi = cross_conj(top)
    re, im = dict(top[0]), dict(top[1])
    for j in range(3):
        re[2, j] = det[0] * wr[j] - det[1] * wi[j]
        im[2, j] = det[0] * wi[j] + det[1] * wr[j]
    return re, im


TOP = [(i, j) for i in range(2) for j in range(3)]


def packed(top, det):
    return [top[0][e] for e in TOP] + [top[1][e] for e in TOP] + list(det)


def unpacked(v):
    top = ({e: v[n] for n, e in enumerate(TOP)}, {e: v[6 + n] for n, e in enumerate(TOP)})
    return top, (v[12], v[13])


def det_product(a, b):
    return a[0] * b[0] - a[1] * b[1], a[0] * b[1] + a[1] * b[0]


def put(ref, lead, count, values):
    for k, v in enumerate(values):
        ref[lead + (pl.ds(k, count, stride=PACK), slice(None))] = v


def get(ref, lead, count):
    return unpacked(
        [ref[lead + (pl.ds(k, count, stride=PACK), slice(None))] for k in range(14)]
    )


def kernel(
    sizes,
    time_in, space_in, gauge_out, fixed_out, profile_out, mean_out,
    tb, sb, gb, fb, halo_s, halo_g, pbuf, buf1, tot, buf2, obuf, gbuf, msg, m1, m2, m3,
    in_sem, out_sem, s1, r1, s2, r2, s3, r3, hs_sem, hg_sem, ms1, mr1, ms2, mr2, ms3, mr3,
):
    steps, layers, n_gz, n_lo, n_hi = sizes
    rows = tb.shape[-2]
    part = rows // n_lo
    size = part * PACK
    ta, gz = lax.axis_index("ta"), lax.axis_index("gz")
    hi, lo = ta // n_lo, ta % n_lo

    load_t = pltpu.make_async_copy(time_in, tb, in_sem.at[0])
    load_t.start()
    load_s = pltpu.make_async_copy(space_in, sb, in_sem.at[1])
    load_s.start()

    def lo_at(d):
        return hi * n_lo + (lo + d) % n_lo

    def gz_at(d):
        return (gz + d) % n_gz

    def hi_at(d):
        return ((hi + d) % n_hi) * n_lo + lo

    barrier = pltpu.get_barrier_semaphore()
    for d in range(1, n_gz):
        pl.semaphore_signal(barrier, inc=1, device_id=(ta, gz_at(d)), device_id_type=MESH)
    for d in range(1, n_lo):
        pl.semaphore_signal(barrier, inc=1, device_id=(lo_at(d), gz), device_id_type=MESH)
    for d in range(1, n_hi):
        pl.semaphore_signal(barrier, inc=1, device_id=(hi_at(d), gz), device_id_type=MESH)

    def matrix(ref, lead, t):
        re = {(i, j): ref[lead + (0, i, j, t)] for i in range(3) for j in range(3)}
        im = {(i, j): ref[lead + (1, i, j, t)] for i in range(3) for j in range(3)}
        return re, im

    def remote(src, dst, send, recv, device):
        return pltpu.make_async_remote_copy(
            src_ref=src, dst_ref=dst, send_sem=send, recv_sem=recv,
            device_id=device, device_id_type=MESH,
        )

    lane = lax.broadcasted_iota(jnp.int32, (rows, LANES), 1)
    row = lax.broadcasted_iota(jnp.int32, (rows, LANES), 0)
    last_x = lane >= LANES - Y
    last_y = lane % Y == Y - 1
    last_z = row % layers == layers - 1

    def step_x(v):
        r = pltpu.roll(v, LANES - Y, 1)
        return jnp.where(last_x, pltpu.roll(r, rows - layers, 0), r)

    def step_y(v):
        return jnp.where(last_y, pltpu.roll(v, Y - 1, 1), pltpu.roll(v, LANES - 1, 1))

    def step_z(v, upper):
        return jnp.where(last_z, pltpu.roll(upper, layers - 1, 0), pltpu.roll(v, rows - 1, 0))

    def moved(f, *ms):
        return tuple({e: f(*(m[c][e] for m in ms)) for e in ms[0][c]} for c in range(2))

    load_t.wait()
    local = matrix(tb, (), 0)
    for t in range(1, steps):
        local = product(local, matrix(tb, (), t))
    put(pbuf, (), rows, packed(local, determinant(local)))

    pl.semaphore_wait(barrier, n_gz - 1 + n_lo - 1 + n_hi - 1)

    def mine(d):
        return pl.ds(pl.multiple_of(((lo + d) % n_lo) * size, 8), size)

    first = [pltpu.make_async_copy(pbuf.at[mine(0)], buf1.at[lo], s1.at[0])]
    for d in range(1, n_lo):
        first.append(remote(pbuf.at[mine(d)], buf1.at[lo], s1.at[d], r1.at[d], (lo_at(d), gz)))
    for c in first[1:] + first[:1]:
        c.start()
    load_s.wait()
    halo_link = remote(
        sb.at[pl.ds(0, 2)], halo_s, hs_sem.at[0], hs_sem.at[1], (ta, gz_at(n_gz - 1))
    )
    halo_link.start()

    def plaquette(a, b_moved, a_moved, b):
        u, v = product(a, b_moved), product(b, a_moved)
        re = sum(u[0][e] * v[0][e] + u[1][e] * v[1][e] for e in u[0])
        return 1.0 - re / 3.0

    density = []
    for t in range(steps):
        x, y = matrix(sb, (0,), t), matrix(sb, (1,), t)
        density.append(plaquette(x, moved(step_x, y), moved(step_y, x), y))
    halo_link.wait_recv()
    for t in range(steps):
        z = matrix(sb, (2,), t)
        for mu, step in ((0, step_x), (1, step_y)):
            a = matrix(sb, (mu,), t)
            up = moved(step_z, a, matrix(halo_s, (mu,), t))
            density[t] = density[t] + plaquette(a, moved(step, z), up, z)
    sites = rows // layers * LANES
    total = None
    for t in range(steps):
        per_row = jnp.broadcast_to(jnp.sum(density[t], axis=1, keepdims=True), (rows, LANES))
        spread = jnp.where(row % layers == lane, per_row, 0.0)
        line = jnp.sum(spread, axis=0, keepdims=True)
        profile_out[t : t + 1, :] = line[:, :layers] / float(sites) / 3.0
        total = per_row if total is None else total + per_row
    total = jnp.broadcast_to(jnp.sum(total, axis=0, keepdims=True), (rows, LANES))

    def spread_sum(n, stage, buf, me, send, recv, device):
        buf[me] = total_at[0]
        msg[stage] = total_at[0]
        out = [
            remote(msg.at[stage], buf.at[me], send.at[d], recv.at[d], device(d))
            for d in range(1, n)
        ]
        for c in out:
            c.start()
        return out

    def gather_sum(n, stage, buf, me, send, recv, device):
        for d in range(1, n):
            remote(
                msg.at[stage], buf.at[(me + n - d) % n], send.at[d], recv.at[d], device(d)
            ).wait_recv()
        got = buf[0]
        for k in range(1, n):
            got = got + buf[k]
        total_at[0] = got

    total_at = [total]
    stage1 = (n_gz, 0, m1, gz, ms1, mr1, lambda d: (ta, gz_at(d)))
    stage2 = (n_lo, 1, m2, lo, ms2, mr2, lambda d: (lo_at(d), gz))
    stage3 = (n_hi, 2, m3, hi, ms3, mr3, lambda d: (hi_at(d), gz))
    sent = spread_sum(*stage1)

    first[0].wait()
    for d in range(1, n_lo):
        remote(
            pbuf.at[mine(d)], buf1.at[(lo + n_lo - d) % n_lo], s1.at[d], r1.at[d], (lo_at(d), gz)
        ).wait_recv()
    before = [None]
    run, run_det = get(buf1, (0,), part)
    for k in range(1, n_lo):
        before.append((run, run_det))
        nxt, nxt_det = get(buf1, (k,), part)
        run = product(run, with_last_row(nxt, nxt_det), rows=(0, 1))
        run_det = det_product(run_det, nxt_det)
    put(tot, (), part, packed(run, run_det))

    def second(d, slot):
        return remote(tot, buf2.at[slot], s2.at[d], r2.at[d], (hi_at(d), gz))

    for d in range(1, n_hi):
        pl.when(hi + d < n_hi)(second(d, hi).start)
    gather_sum(*stage1)
    sent += spread_sum(*stage2)
    gather_sum(*stage2)
    sent += spread_sum(*stage3)
    full_before = [None] + [with_last_row(*b) for b in before[1:]]
    for d in range(1, n_hi):
        pl.when(hi >= d)(second(d, (hi + n_hi - d) % n_hi).wait_recv)

    zero = jnp.zeros((part, LANES), jnp.float32)
    one = jnp.ones((part, LANES), jnp.float32)
    acc = ({e: one if e[0] == e[1] else zero for e in TOP}, {e: zero for e in TOP})
    acc_det = (one, zero)
    for k in range(n_hi - 1):
        nxt, nxt_det = get(buf2, (k,), part)
        if k == 0:
            new, new_det = nxt, nxt_det
        else:
            new = product(acc, with_last_row(nxt, nxt_det), rows=(0, 1))
            new_det = det_product(acc_det, nxt_det)
        use = k < hi
        acc = moved(lambda n, o: jnp.where(use, n, o), new, acc)
        acc_det = tuple(jnp.where(use, n, o) for n, o in zip(new_det, acc_det))

    put(obuf, (0,), part, packed(acc, acc_det))
    for k in range(1, n_lo):
        top = product(acc, full_before[k], rows=(0, 1))
        put(obuf, (k,), part, packed(top, det_product(acc_det, before[k][1])))
    third = [pltpu.make_async_copy(obuf.at[lo], gbuf.at[mine(0)], s3.at[0])]
    for d in range(1, n_lo):
        third.append(
            remote(obuf.at[(lo + d) % n_lo], gbuf.at[mine(0)], s3.at[d], r3.at[d], (lo_at(d), gz))
        )
    for c in third[1:] + third[:1]:
        c.start()
    third[0].wait()
    for d in range(1, n_lo):
        remote(
            obuf.at[(lo + d) % n_lo], gbuf.at[mine(n_lo - d)], s3.at[d], r3.at[d], (lo_at(d), gz)
        ).wait_recv()

    def keep(ref, lead, t, m):
        for i in range(3):
            for j in range(3):
                ref[lead + (0, i, j, t)] = m[0][i, j]
                ref[lead + (1, i, j, t)] = m[1][i, j]

    gauge = with_last_row(*get(gbuf, (), rows))
    for t in range(steps):
        keep(gb, (), t, gauge)
        if t < steps - 1:
            gauge = product(gauge, matrix(tb, (), t))
    halo_gauge = remote(gb, halo_g, hg_sem.at[0], hg_sem.at[1], (ta, gz_at(n_gz - 1)))
    halo_gauge.start()
    stores = [pltpu.make_async_copy(gb, gauge_out, out_sem.at[0])]
    stores[0].start()

    for mu in range(3):
        if mu == 2:
            halo_gauge.wait_recv()
        for t in range(steps):
            g = matrix(gb, (), t)
            if mu == 2:
                ahead = moved(step_z, g, matrix(halo_g, (), t))
            else:
                ahead = moved((step_x, step_y)[mu], g)
            keep(fb, (mu,), t, product_dagger(product(g, matrix(sb, (mu,), t)), ahead))
        stores.append(pltpu.make_async_copy(fb.at[mu], fixed_out.at[mu], out_sem.at[1 + mu]))
        stores[-1].start()

    gather_sum(*stage3)
    count = sites * 3.0 * steps * layers * n_gz * n_lo * n_hi
    mean_out[...] = total_at[0][0:1, 0:1] / count

    for c in first[1:] + third[1:] + sent + [halo_link, halo_gauge]:
        c.wait_send()
    for d in range(1, n_hi):
        pl.when(hi + d < n_hi)(second(d, hi).wait_send)
    for c in stores:
        c.wait()


def on_device(n_ta, n_gz, time_links, space_links):
    steps, layers, sites = time_links.shape[3:]
    n_lo = 1
    while n_lo * 2 * n_lo * 2 <= n_ta:
        n_lo *= 2
    n_hi = n_ta // n_lo
    t_rows, s_rows = to_rows(time_links), to_rows(space_links)
    rows = t_rows.shape[-2]
    size = rows // n_lo * PACK
    f32 = jnp.float32
    dma = pltpu.SemaphoreType.DMA
    anywhere = pl.BlockSpec(memory_space=pl.ANY)
    vmem = pl.BlockSpec(memory_space=pltpu.VMEM)
    gauge, fixed, profile, mean = pl.pallas_call(
        functools.partial(kernel, (steps, layers, n_gz, n_lo, n_hi)),
        out_shape=[
            jax.ShapeDtypeStruct(t_rows.shape, f32),
            jax.ShapeDtypeStruct(s_rows.shape, f32),
            jax.ShapeDtypeStruct((steps, layers), f32),
            jax.ShapeDtypeStruct((1, 1), f32),
        ],
        in_specs=[anywhere, anywhere],
        out_specs=[anywhere, anywhere, vmem, vmem],
        scratch_shapes=[
            pltpu.VMEM(t_rows.shape, f32),
            pltpu.VMEM(s_rows.shape, f32),
            pltpu.VMEM(t_rows.shape, f32),
            pltpu.VMEM(s_rows.shape, f32),
            pltpu.VMEM((2,) + s_rows.shape[1:], f32),
            pltpu.VMEM(t_rows.shape, f32),
            pltpu.VMEM((rows * PACK, LANES), f32),
            pltpu.VMEM((n_lo, size, LANES), f32),
            pltpu.VMEM((size, LANES), f32),
            pltpu.VMEM((n_hi, size, LANES), f32),
            pltpu.VMEM((n_lo, size, LANES), f32),
            pltpu.VMEM((rows * PACK, LANES), f32),
            pltpu.VMEM((3, rows, LANES), f32),
            pltpu.VMEM((n_gz, rows, LANES), f32),
            pltpu.VMEM((n_lo, rows, LANES), f32),
            pltpu.VMEM((n_hi, rows, LANES), f32),
            dma((2,)), dma((4,)),
            dma((n_lo,)), dma((n_lo,)), dma((n_hi,)), dma((n_hi,)), dma((n_lo,)), dma((n_lo,)),
            dma((2,)), dma((2,)),
            dma((n_gz,)), dma((n_gz,)), dma((n_lo,)), dma((n_lo,)), dma((n_hi,)), dma((n_hi,)),
        ],
        compiler_params=pltpu.CompilerParams(collective_id=0, has_side_effects=True),
    )(t_rows, s_rows)
    return (
        from_rows(gauge, layers, sites),
        from_rows(fixed, layers, sites),
        profile,
        mean.reshape(()),
    )


def solution(mesh):
    return jax.shard_map(
        functools.partial(on_device, mesh.shape["ta"], mesh.shape["gz"]),
        mesh=mesh,
        in_specs=(
            P(None, None, None, "ta", "gz", None),
            P(None, None, None, None, "ta", "gz", None),
        ),
        out_specs=(
            P(None, None, None, "ta", "gz", None),
            P(None, None, None, None, "ta", "gz", None),
            P("ta", "gz"),
            P(),
        ),
        check_vma=False,
    )
```

time: 150 us -> 25.1 us (0.17)
  the two profiles are of different devices: /device:TPU:0 before, /device:TPU:1 now
where the time goes in v1:
time: 25.1 us; the launch traced here: 24.9 us
  Pallas kernels  18.6 us (74%)
  local copies, waits for them, and re-layouts  3.95 us (16%)
  between operations  2.34 us (9%)
    pallas_call x1, Pallas kernels, on_device(): pl.pallas_call(functools.partial(kernel, (steps, layers, n_gz, n_lo, n_hi...  18.6 us
    unnamed x5, local copies, waits for them, and re-layouts  3.95 us

profile of v1, /device:TPU:1, one launch (start us, length us, event | category | flops | bytes accessed | tf_op | source)
XLA Modules:
  0.0 24.9 jit_solution(372056886667806180)
XLA Ops:
  0.6 18.6 %shard_map.57 = (f32[2,3,3,2,8,128]{5,4,3,2,1,0:T(8,128)}, f32[3,2,3,3,2,8,128]{6,5,4,3,2,1,0:T(8,128)}, f32[2,4]{1,0:T(2,128)}, f32[1,1]{1,0:T(1,128)}) custom-call(f32[2,3,3,2,8,128]{5,4,3,2,1,0:T(8,128)} %bitcast.24, f32[3,2,3,3,2,8,128]{6,5,4,3,2,1,0:T(8,128)} %bitcast.22), custom_call_target="tpu_custom_call" | custom-call | tf_op jit(solution)/shard_map/pallas_call | solution.py:370
  19.3 1.6 %copy.14 = f32[2,3,3,2,4,256]{5,4,3,2,1,0:T(4,128)} copy(f32[2,3,3,2,4,256]{5,4,3,2,1,0:T(4,128)} %bitcast.23) | data formatting | bytes 294912
  20.8 0.0 copy-start
  20.8 1.8 %copy.15 = f32[3,2,3,3,2,4,256]{6,5,4,3,2,1,0:T(4,128)} copy(f32[3,2,3,3,2,4,256]{6,5,4,3,2,1,0:T(4,128)} %bitcast.21) | data formatting | bytes 884736
  22.6 0.0 copy-done
  22.6 0.6 %copy.16 = f32[2,4]{1,0:T(2,128)} copy(f32[2,4]{1,0:T(2,128)S(1)} %copy-done) | data formatting | bytes 64
Async XLA Ops:
  20.8 1.8 %copy-start = (f32[2,4]{1,0:T(2,128)S(1)}, f32[2,4]{1,0:T(2,128)}, u32[]{:S(2)}) copy-start(f32[2,4]{1,0:T(2,128)} %get-tuple-element.18) | copy-start | bytes 100

commit v2 on v1

--- a/solution.py
+++ b/solution.py
@@ -10,6 +10,7 @@
 X = 16
 Y = 16
 LANES = 128
+GRANT = 8 << 20
 MESH = pl.DeviceIdType.MESH
 PACK = 16
 
@@ -114,11 +115,48 @@
     )
 
 
-def kernel(
+def matrix(ref, lead, t):
+    re = {(i, j): ref[lead + (0, i, j, t)] for i in range(3) for j in range(3)}
+    im = {(i, j): ref[lead + (1, i, j, t)] for i in range(3) for j in range(3)}
+    return re, im
+
+
+def keep(ref, lead, t, m):
+    for i in range(3):
+        for j in range(3):
+            ref[lead + (0, i, j, t)] = m[0][i, j]
+            ref[lead + (1, i, j, t)] = m[1][i, j]
+
+
+def moved(f, *ms):
+    return tuple({e: f(*(m[c][e] for m in ms)) for e in ms[0][c]} for c in range(2))
+
+
+def steppers(rows, layers):
+    lane = lax.broadcasted_iota(jnp.int32, (rows, LANES), 1)
+    row = lax.broadcasted_iota(jnp.int32, (rows, LANES), 0)
+    last_x = lane >= LANES - Y
+    last_y = lane % Y == Y - 1
+    last_z = row % layers == layers - 1
+
+    def step_x(v):
+        r = pltpu.roll(v, LANES - Y, 1)
+        return jnp.where(last_x, pltpu.roll(r, rows - layers, 0), r)
+
+    def step_y(v):
+        return jnp.where(last_y, pltpu.roll(v, Y - 1, 1), pltpu.roll(v, LANES - 1, 1))
+
+    def step_z(v, upper):
+        return jnp.where(last_z, pltpu.roll(upper, layers - 1, 0), pltpu.roll(v, rows - 1, 0))
+
+    return step_x, step_y, step_z, lane, row
+
+
+def scan_kernel(
     sizes,
-    time_in, space_in, gauge_out, fixed_out, profile_out, mean_out,
-    tb, sb, gb, fb, halo_s, halo_g, pbuf, buf1, tot, buf2, obuf, gbuf, msg, m1, m2, m3,
-    in_sem, out_sem, s1, r1, s2, r2, s3, r3, hs_sem, hg_sem, ms1, mr1, ms2, mr2, ms3, mr3,
+    time_in, space_in, gauge_out, above_out, profile_out, mean_out, tb, sb,
+    halo_t, halo_s, pbuf, buf1, tot, buf2, obuf, gbuf, hbuf, msg, m1, m2, m3,
+    in_sem, s1, r1, s2, r2, s3, r3, s4, r4, hs_sem, ht_sem, ms1, mr1, ms2, mr2, ms3, mr3,
 ):
     steps, layers, n_gz, n_lo, n_hi = sizes
     rows = tb.shape[-2]
@@ -132,8 +170,16 @@
     load_s = pltpu.make_async_copy(space_in, sb, in_sem.at[1])
     load_s.start()
 
-    def lo_at(d):
-        return hi * n_lo + (lo + d) % n_lo
+    def flip(m):
+        out, bit = 0, 1
+        while bit < n_lo:
+            b = (lo // bit) % 2
+            out = out + bit * (1 - b if m & bit else b)
+            bit *= 2
+        return out
+
+    def lo_at(m):
+        return hi * n_lo + flip(m)
 
     def gz_at(d):
         return (gz + d) % n_gz
@@ -148,11 +194,12 @@
         pl.semaphore_signal(barrier, inc=1, device_id=(lo_at(d), gz), device_id_type=MESH)
     for d in range(1, n_hi):
         pl.semaphore_signal(barrier, inc=1, device_id=(hi_at(d), gz), device_id_type=MESH)
-
-    def matrix(ref, lead, t):
-        re = {(i, j): ref[lead + (0, i, j, t)] for i in range(3) for j in range(3)}
-        im = {(i, j): ref[lead + (1, i, j, t)] for i in range(3) for j in range(3)}
-        return re, im
+    near = sorted({1, n_gz - 1})
+    for g in near:
+        for d in range(1, n_lo):
+            pl.semaphore_signal(
+                barrier, inc=1, device_id=(lo_at(d), gz_at(g)), device_id_type=MESH
+            )
 
     def remote(src, dst, send, recv, device):
         return pltpu.make_async_remote_copy(
@@ -160,24 +207,7 @@
             device_id=device, device_id_type=MESH,
         )
 
-    lane = lax.broadcasted_iota(jnp.int32, (rows, LANES), 1)
-    row = lax.broadcasted_iota(jnp.int32, (rows, LANES), 0)
-    last_x = lane >= LANES - Y
-    last_y = lane % Y == Y - 1
-    last_z = row % layers == layers - 1
-
-    def step_x(v):
-        r = pltpu.roll(v, LANES - Y, 1)
-        return jnp.where(last_x, pltpu.roll(r, rows - layers, 0), r)
-
-    def step_y(v):
-        return jnp.where(last_y, pltpu.roll(v, Y - 1, 1), pltpu.roll(v, LANES - 1, 1))
-
-    def step_z(v, upper):
-        return jnp.where(last_z, pltpu.roll(upper, layers - 1, 0), pltpu.roll(v, rows - 1, 0))
-
-    def moved(f, *ms):
-        return tuple({e: f(*(m[c][e] for m in ms)) for e in ms[0][c]} for c in range(2))
+    step_x, step_y, step_z, lane, row = steppers(rows, layers)
 
     load_t.wait()
     local = matrix(tb, (), 0)
@@ -185,21 +215,26 @@
         local = product(local, matrix(tb, (), t))
     put(pbuf, (), rows, packed(local, determinant(local)))
 
-    pl.semaphore_wait(barrier, n_gz - 1 + n_lo - 1 + n_hi - 1)
+    pl.semaphore_wait(barrier, n_gz - 1 + (n_lo - 1) * (1 + len(near)) + n_hi - 1)
 
     def mine(d):
-        return pl.ds(pl.multiple_of(((lo + d) % n_lo) * size, 8), size)
-
+        return pl.ds(pl.multiple_of(flip(d) * size, 8), size)
+
+    far_first = sorted(range(1, n_lo), key=lambda m: -bin(m).count("1"))
     first = [pltpu.make_async_copy(pbuf.at[mine(0)], buf1.at[lo], s1.at[0])]
-    for d in range(1, n_lo):
+    for d in far_first:
         first.append(remote(pbuf.at[mine(d)], buf1.at[lo], s1.at[d], r1.at[d], (lo_at(d), gz)))
     for c in first[1:] + first[:1]:
         c.start()
     load_s.wait()
-    halo_link = remote(
-        sb.at[pl.ds(0, 2)], halo_s, hs_sem.at[0], hs_sem.at[1], (ta, gz_at(n_gz - 1))
+    below = gz_at(n_gz - 1)
+    halo_link = remote(sb.at[pl.ds(0, 2)], halo_s, hs_sem.at[0], hs_sem.at[1], (ta, below))
+    halo_link.start()
+    halo_time = remote(
+        tb.at[:, :, :, pl.ds(0, steps - 1)], halo_t, ht_sem.at[0], ht_sem.at[1], (ta, below)
     )
-    halo_link.start()
+    if steps > 1:
+        halo_time.start()
 
     def plaquette(a, b_moved, a_moved, b):
         u, v = product(a, b_moved), product(b, a_moved)
@@ -227,7 +262,7 @@
         total = per_row if total is None else total + per_row
     total = jnp.broadcast_to(jnp.sum(total, axis=0, keepdims=True), (rows, LANES))
 
-    def spread_sum(n, stage, buf, me, send, recv, device):
+    def spread_sum(n, stage, buf, me, send, recv, device, source):
         buf[me] = total_at[0]
         msg[stage] = total_at[0]
         out = [
@@ -238,10 +273,10 @@
             c.start()
         return out
 
-    def gather_sum(n, stage, buf, me, send, recv, device):
+    def gather_sum(n, stage, buf, me, send, recv, device, source):
         for d in range(1, n):
             remote(
-                msg.at[stage], buf.at[(me + n - d) % n], send.at[d], recv.at[d], device(d)
+                msg.at[stage], buf.at[source(d)], send.at[d], recv.at[d], device(d)
             ).wait_recv()
         got = buf[0]
         for k in range(1, n):
@@ -249,15 +284,15 @@
         total_at[0] = got
 
     total_at = [total]
-    stage1 = (n_gz, 0, m1, gz, ms1, mr1, lambda d: (ta, gz_at(d)))
-    stage2 = (n_lo, 1, m2, lo, ms2, mr2, lambda d: (lo_at(d), gz))
-    stage3 = (n_hi, 2, m3, hi, ms3, mr3, lambda d: (hi_at(d), gz))
+    stage1 = (n_gz, 0, m1, gz, ms1, mr1, lambda d: (ta, gz_at(d)), lambda d: gz_at(n_gz - d))
+    stage2 = (n_lo, 1, m2, lo, ms2, mr2, lambda d: (lo_at(d), gz), flip)
+    stage3 = (n_hi, 2, m3, hi, ms3, mr3, lambda d: (hi_at(d), gz), lambda d: (hi + n_hi - d) % n_hi)
     sent = spread_sum(*stage1)
 
     first[0].wait()
     for d in range(1, n_lo):
         remote(
-            pbuf.at[mine(d)], buf1.at[(lo + n_lo - d) % n_lo], s1.at[d], r1.at[d], (lo_at(d), gz)
+            pbuf.at[mine(d)], buf1.at[flip(d)], s1.at[d], r1.at[d], (lo_at(d), gz)
         ).wait_recv()
     before = [None]
     run, run_det = get(buf1, (0,), part)
@@ -271,7 +306,7 @@
     def second(d, slot):
         return remote(tot, buf2.at[slot], s2.at[d], r2.at[d], (hi_at(d), gz))
 
-    for d in range(1, n_hi):
+    for d in reversed(range(1, n_hi)):
         pl.when(hi + d < n_hi)(second(d, hi).start)
     gather_sum(*stage1)
     sent += spread_sum(*stage2)
@@ -301,55 +336,89 @@
         top = product(acc, full_before[k], rows=(0, 1))
         put(obuf, (k,), part, packed(top, det_product(acc_det, before[k][1])))
     third = [pltpu.make_async_copy(obuf.at[lo], gbuf.at[mine(0)], s3.at[0])]
-    for d in range(1, n_lo):
+    for d in far_first:
         third.append(
-            remote(obuf.at[(lo + d) % n_lo], gbuf.at[mine(0)], s3.at[d], r3.at[d], (lo_at(d), gz))
+            remote(obuf.at[flip(d)], gbuf.at[mine(0)], s3.at[d], r3.at[d], (lo_at(d), gz))
         )
-    for c in third[1:] + third[:1]:
+    lowest = (lo * part) % layers == 0
+
+    def fourth(d, source):
+        rows_there = pl.ds(pl.multiple_of(source * size, 8), PACK)
+        return remote(
+            obuf.at[flip(d), pl.ds(0, PACK)], hbuf.at[rows_there], s4.at[d], r4.at[source],
+            (lo_at(d), below),
+        )
+
+    for c in third[1:]:
         c.start()
+    for d in far_first + [0]:
+        pl.when(lowest)(fourth(d, lo).start)
+    third[0].start()
+    if steps > 1:
+        halo_time.wait_recv()
+    gather_sum(*stage3)
+    count = sites * 3.0 * steps * layers * n_gz * n_lo * n_hi
+    mean_out[...] = total_at[0] / count
     third[0].wait()
     for d in range(1, n_lo):
         remote(
-            obuf.at[(lo + d) % n_lo], gbuf.at[mine(n_lo - d)], s3.at[d], r3.at[d], (lo_at(d), gz)
+            obuf.at[flip(d)], gbuf.at[mine(d)], s3.at[d], r3.at[d], (lo_at(d), gz)
         ).wait_recv()
-
-    def keep(ref, lead, t, m):
-        for i in range(3):
-            for j in range(3):
-                ref[lead + (0, i, j, t)] = m[0][i, j]
-                ref[lead + (1, i, j, t)] = m[1][i, j]
-
-    gauge = with_last_row(*get(gbuf, (), rows))
+    for k in range(14):
+        gauge_out[k] = gbuf[pl.ds(k, rows, stride=PACK), :]
+    for k in range(n_lo):
+        if (k * part) % layers == 0:
+            fourth(0, k).wait_recv()
+    above = with_last_row(*get(hbuf, (), rows))
+    for t in range(steps):
+        keep(above_out, (), t, above)
+        if t < steps - 1:
+            above = product(above, matrix(halo_t, (), t))
+
+    for c in first[1:] + third[1:] + sent + [halo_link]:
+        c.wait_send()
+    if steps > 1:
+        halo_time.wait_send()
+    for d in range(n_lo):
+        pl.when(lowest)(fourth(d, lo).wait_send)
+    for d in range(1, n_hi):
+        pl.when(hi + d < n_hi)(second(d, hi).wait_send)
+
+
+def fix_kernel(
+    sizes,
+    packed_in, above_in, profile_in, mean_in, tb, sb,
+    gauge_out, fixed_out, profile_out, mean_out,
+    gb, fb, pb, mb, out_sem,
+):
+    steps, layers = sizes
+    rows = tb.shape[-2]
+    pb[...] = profile_in[...]
+    mb[...] = mean_in[0:1, 0:1]
+    stores = [
+        pltpu.make_async_copy(pb, profile_out, out_sem.at[4]),
+        pltpu.make_async_copy(mb, mean_out, out_sem.at[5]),
+    ]
+    for c in stores:
+        c.start()
+    step_x, step_y, step_z, _, _ = steppers(rows, layers)
+    gauge = with_last_row(*unpacked([packed_in[k] for k in range(14)]))
     for t in range(steps):
         keep(gb, (), t, gauge)
         if t < steps - 1:
             gauge = product(gauge, matrix(tb, (), t))
-    halo_gauge = remote(gb, halo_g, hg_sem.at[0], hg_sem.at[1], (ta, gz_at(n_gz - 1)))
-    halo_gauge.start()
-    stores = [pltpu.make_async_copy(gb, gauge_out, out_sem.at[0])]
-    stores[0].start()
-
+    stores.append(pltpu.make_async_copy(gb, gauge_out, out_sem.at[3]))
+    stores[-1].start()
     for mu in range(3):
-        if mu == 2:
-            halo_gauge.wait_recv()
         for t in range(steps):
             g = matrix(gb, (), t)
             if mu == 2:
-                ahead = moved(step_z, g, matrix(halo_g, (), t))
+                ahead = moved(step_z, g, matrix(above_in, (), t))
             else:
                 ahead = moved((step_x, step_y)[mu], g)
             keep(fb, (mu,), t, product_dagger(product(g, matrix(sb, (mu,), t)), ahead))
-        stores.append(pltpu.make_async_copy(fb.at[mu], fixed_out.at[mu], out_sem.at[1 + mu]))
+        stores.append(pltpu.make_async_copy(fb.at[mu], fixed_out.at[mu], out_sem.at[mu]))
         stores[-1].start()
-
-    gather_sum(*stage3)
-    count = sites * 3.0 * steps * layers * n_gz * n_lo * n_hi
-    mean_out[...] = total_at[0][0:1, 0:1] / count
-
-    for c in first[1:] + third[1:] + sent + [halo_link, halo_gauge]:
-        c.wait_send()
-    for d in range(1, n_hi):
-        pl.when(hi + d < n_hi)(second(d, hi).wait_send)
     for c in stores:
         c.wait()
 
@@ -365,42 +434,54 @@
     size = rows // n_lo * PACK
     f32 = jnp.float32
     dma = pltpu.SemaphoreType.DMA
-    anywhere = pl.BlockSpec(memory_space=pl.ANY)
     vmem = pl.BlockSpec(memory_space=pltpu.VMEM)
-    gauge, fixed, profile, mean = pl.pallas_call(
-        functools.partial(kernel, (steps, layers, n_gz, n_lo, n_hi)),
+    some = lambda shape: jax.ShapeDtypeStruct(shape, f32)
+    halo_shape = t_rows.shape[:3] + (max(steps - 1, 1),) + t_rows.shape[4:]
+    packed_gauge, above, profile, mean, held_t, held_s = pl.pallas_call(
+        functools.partial(scan_kernel, (steps, layers, n_gz, n_lo, n_hi)),
         out_shape=[
-            jax.ShapeDtypeStruct(t_rows.shape, f32),
-            jax.ShapeDtypeStruct(s_rows.shape, f32),
-            jax.ShapeDtypeStruct((steps, layers), f32),
-            jax.ShapeDtypeStruct((1, 1), f32),
+            some((14, rows, LANES)), some(t_rows.shape), some((steps, layers)),
+            some((rows, LANES)), some(t_rows.shape), some(s_rows.shape),
         ],
-        in_specs=[anywhere, anywhere],
-        out_specs=[anywhere, anywhere, vmem, vmem],
+        in_specs=[pl.BlockSpec(memory_space=pltpu.HBM)] * 2,
+        out_specs=[vmem] * 6,
         scratch_shapes=[
-            pltpu.VMEM(t_rows.shape, f32),
-            pltpu.VMEM(s_rows.shape, f32),
-            pltpu.VMEM(t_rows.shape, f32),
-            pltpu.VMEM(s_rows.shape, f32),
+            pltpu.VMEM(halo_shape, f32),
             pltpu.VMEM((2,) + s_rows.shape[1:], f32),
-            pltpu.VMEM(t_rows.shape, f32),
             pltpu.VMEM((rows * PACK, LANES), f32),
             pltpu.VMEM((n_lo, size, LANES), f32),
             pltpu.VMEM((size, LANES), f32),
             pltpu.VMEM((n_hi, size, LANES), f32),
             pltpu.VMEM((n_lo, size, LANES), f32),
             pltpu.VMEM((rows * PACK, LANES), f32),
+            pltpu.VMEM((rows * PACK, LANES), f32),
             pltpu.VMEM((3, rows, LANES), f32),
             pltpu.VMEM((n_gz, rows, LANES), f32),
             pltpu.VMEM((n_lo, rows, LANES), f32),
             pltpu.VMEM((n_hi, rows, LANES), f32),
-            dma((2,)), dma((4,)),
+            dma((2,)),
             dma((n_lo,)), dma((n_lo,)), dma((n_hi,)), dma((n_hi,)), dma((n_lo,)), dma((n_lo,)),
-            dma((2,)), dma((2,)),
+            dma((n_lo,)), dma((n_lo,)), dma((2,)), dma((2,)),
             dma((n_gz,)), dma((n_gz,)), dma((n_lo,)), dma((n_lo,)), dma((n_hi,)), dma((n_hi,)),
         ],
-        compiler_params=pltpu.CompilerParams(collective_id=0, has_side_effects=True),
-    )(t_rows, s_rows)
+        compiler_params=pltpu.CompilerParams(
+            collective_id=0, has_side_effects=True, vmem_limit_bytes=GRANT
+        ),
+    )(*(pltpu.with_memory_space_constraint(a, pltpu.HBM) for a in (t_rows, s_rows)))
+    gauge, fixed, profile, mean = pl.pallas_call(
+        functools.partial(fix_kernel, (steps, layers)),
+        out_shape=[some(t_rows.shape), some(s_rows.shape), some((steps, layers)), some((1, 1))],
+        in_specs=[vmem] * 6,
+        out_specs=[pl.BlockSpec(memory_space=pltpu.HBM)] * 4,
+        scratch_shapes=[
+            pltpu.VMEM(t_rows.shape, f32),
+            pltpu.VMEM(s_rows.shape, f32),
+            pltpu.VMEM((steps, layers), f32),
+            pltpu.VMEM((1, 1), f32),
+            dma((6,)),
+        ],
+        compiler_params=pltpu.CompilerParams(vmem_limit_bytes=GRANT),
+    )(packed_gauge, above, profile, mean, held_t, held_s)
     return (
         from_rows(gauge, layers, sites),
         from_rows(fixed, layers, sites),

time: 25.1 us -> 18.6 us (0.74)
  the two profiles are of different devices: /device:TPU:1 before, /device:TPU:0 now
where the time goes in v2:
time: 18.6 us; the launch traced here: 18.4 us
  Pallas kernels  17.8 us (96%)
  between operations  0.64 us (3%)
    pallas_call x1, Pallas kernels, on_device(): pl.pallas_call(functools.partial(scan_kernel, (steps, layers, n_gz, n_lo,...  16.5 us
    pallas_call x1, Pallas kernels, on_device(): pl.pallas_call(functools.partial(fix_kernel, (steps, layers)), out_shape=...  1.29 us

profile of v2, /device:TPU:0, one launch (start us, length us, event | category | flops | bytes accessed | tf_op | source)
XLA Modules:
  0.0 18.4 jit_solution(7280247750582562499)
XLA Ops:
  0.6 16.5 %shard_map.57 = (f32[14,8,128]{2,1,0:T(8,128)S(1)}, f32[2,3,3,2,8,128]{5,4,3,2,1,0:T(8,128)S(1)}, f32[2,4]{1,0:T(2,128)S(1)}, f32[8,128]{1,0:T(8,128)S(1)}, f32[...) custom-call(f32[2,3,3,2,8,128]{5,4,3,2,1,0:T(8,128)} %bitcast.22, ...), custom_call_target="tpu_custom_call" | custom-call | tf_op jit(solution)/shard_map/pallas_call | solution.py:440
  17.1 1.3 %shard_map.58 = (f32[2,3,3,2,8,128]{5,4,3,2,1,0:T(8,128)}, f32[3,2,3,3,2,8,128]{6,5,4,3,2,1,0:T(8,128)}, f32[2,4]{1,0:T(2,128)}, f32[1,1]{1,0:T(1,128)}) custom-call(f32[14,8,128]{2,1,0:T(8,128)S(1)} %get-tuple-element.14.packed_in, f32[2,3,3,2,8,128]{5,4,3,2,1,0:T(8,128)S(1)} %get-tuple-element.15.above_in, f32[2,4]{1,0:T(2,128)S(1)} %get-tuple-element.16.profile_in, ...), custom_call_target="tpu_custom_call" | custom-call | tf_op jit(solution)/shard_map/pallas_call | solution.py:471

commit v3 on v2

--- a/solution.py
+++ b/solution.py
@@ -157,6 +157,7 @@
     time_in, space_in, gauge_out, above_out, profile_out, mean_out, tb, sb,
     halo_t, halo_s, pbuf, buf1, tot, buf2, obuf, gbuf, hbuf, msg, m1, m2, m3,
     in_sem, s1, r1, s2, r2, s3, r3, s4, r4, hs_sem, ht_sem, ms1, mr1, ms2, mr2, ms3, mr3,
+    beside_sem, down_sem, up_sem,
 ):
     steps, layers, n_gz, n_lo, n_hi = sizes
     rows = tb.shape[-2]
@@ -192,14 +193,13 @@
         pl.semaphore_signal(barrier, inc=1, device_id=(ta, gz_at(d)), device_id_type=MESH)
     for d in range(1, n_lo):
         pl.semaphore_signal(barrier, inc=1, device_id=(lo_at(d), gz), device_id_type=MESH)
-    for d in range(1, n_hi):
-        pl.semaphore_signal(barrier, inc=1, device_id=(hi_at(d), gz), device_id_type=MESH)
-    near = sorted({1, n_gz - 1})
-    for g in near:
-        for d in range(1, n_lo):
-            pl.semaphore_signal(
-                barrier, inc=1, device_id=(lo_at(d), gz_at(g)), device_id_type=MESH
-            )
+    def tell(sem, device):
+        pl.semaphore_signal(sem, inc=1, device_id=device, device_id_type=MESH)
+
+    next_hi = ((ta + n_lo) % (n_hi * n_lo), gz)
+    last_hi = ((ta + (n_hi - 1) * n_lo) % (n_hi * n_lo), gz)
+    pl.when(hi < n_hi - 1)(lambda: tell(barrier, next_hi))
+    pl.when(hi > 0)(lambda: tell(barrier, last_hi))
 
     def remote(src, dst, send, recv, device):
         return pltpu.make_async_remote_copy(
@@ -215,7 +215,8 @@
         local = product(local, matrix(tb, (), t))
     put(pbuf, (), rows, packed(local, determinant(local)))
 
-    pl.semaphore_wait(barrier, n_gz - 1 + (n_lo - 1) * (1 + len(near)) + n_hi - 1)
+    ends = jnp.where(hi > 0, 1, 0) + jnp.where(hi < n_hi - 1, 1, 0)
+    pl.semaphore_wait(barrier, n_gz - 1 + n_lo - 1 + ends)
 
     def mine(d):
         return pl.ds(pl.multiple_of(flip(d) * size, 8), size)
@@ -226,6 +227,11 @@
         first.append(remote(pbuf.at[mine(d)], buf1.at[lo], s1.at[d], r1.at[d], (lo_at(d), gz)))
     for c in first[1:] + first[:1]:
         c.start()
+    for d in range(1, n_lo):
+        tell(beside_sem, (lo_at(d), gz))
+    if n_hi > 2:
+        pl.when(hi == n_hi - 2)(lambda: tell(down_sem, last_hi))
+        pl.when(hi == 1)(lambda: tell(up_sem, next_hi))
     load_s.wait()
     below = gz_at(n_gz - 1)
     halo_link = remote(sb.at[pl.ds(0, 2)], halo_s, hs_sem.at[0], hs_sem.at[1], (ta, below))
@@ -245,6 +251,11 @@
     for t in range(steps):
         x, y = matrix(sb, (0,), t), matrix(sb, (1,), t)
         density.append(plaquette(x, moved(step_x, y), moved(step_y, x), y))
+    if n_hi > 2:
+        pl.when(hi <= n_hi - 3)(lambda: pl.semaphore_wait(down_sem, 1))
+        pl.when((hi > 0) & (hi <= n_hi - 3))(lambda: tell(down_sem, last_hi))
+        pl.when(hi >= 2)(lambda: pl.semaphore_wait(up_sem, 1))
+        pl.when((hi < n_hi - 1) & (hi >= 2))(lambda: tell(up_sem, next_hi))
     halo_link.wait_recv()
     for t in range(steps):
         z = matrix(sb, (2,), t)
@@ -312,6 +323,7 @@
     sent += spread_sum(*stage2)
     gather_sum(*stage2)
     sent += spread_sum(*stage3)
+    pl.semaphore_wait(beside_sem, n_lo - 1)
     full_before = [None] + [with_last_row(*b) for b in before[1:]]
     for d in range(1, n_hi):
         pl.when(hi >= d)(second(d, (hi + n_hi - d) % n_hi).wait_recv)
@@ -433,7 +445,7 @@
     rows = t_rows.shape[-2]
     size = rows // n_lo * PACK
     f32 = jnp.float32
-    dma = pltpu.SemaphoreType.DMA
+    dma, regular = pltpu.SemaphoreType.DMA, pltpu.SemaphoreType.REGULAR
     vmem = pl.BlockSpec(memory_space=pltpu.VMEM)
     some = lambda shape: jax.ShapeDtypeStruct(shape, f32)
     halo_shape = t_rows.shape[:3] + (max(steps - 1, 1),) + t_rows.shape[4:]
@@ -463,6 +475,7 @@
             dma((n_lo,)), dma((n_lo,)), dma((n_hi,)), dma((n_hi,)), dma((n_lo,)), dma((n_lo,)),
             dma((n_lo,)), dma((n_lo,)), dma((2,)), dma((2,)),
             dma((n_gz,)), dma((n_gz,)), dma((n_lo,)), dma((n_lo,)), dma((n_hi,)), dma((n_hi,)),
+            regular, regular, regular,
         ],
         compiler_params=pltpu.CompilerParams(
             collective_id=0, has_side_effects=True, vmem_limit_bytes=GRANT

time: 18.6 us -> 18.3 us (0.984)
  Pallas kernels: 17.8 us -> 17.5 us
    pallas_call x1, Pallas kernels: 16.5 us -> 16.2 us  [on_device(): pl.pallas_call(functools.partial(scan_kernel, (steps, layers, n_gz, n_lo,...]
where the time goes in v3:
time: 18.3 us; the launch traced here: 18.1 us
  Pallas kernels  17.5 us (96%)
  between operations  0.64 us (3%)
    pallas_call x1, Pallas kernels, on_device(): pl.pallas_call(functools.partial(scan_kernel, (steps, layers, n_gz, n_lo,...  16.2 us
    pallas_call x1, Pallas kernels, on_device(): pl.pallas_call(functools.partial(fix_kernel, (steps, layers)), out_shape=...  1.29 us

profile of v3, /device:TPU:0, one launch (start us, length us, event | category | flops | bytes accessed | tf_op | source)
XLA Modules:
  0.0 18.1 jit_solution(7754220192229324137)
XLA Ops:
  0.6 16.2 %shard_map.57 = (f32[14,8,128]{2,1,0:T(8,128)S(1)}, f32[2,3,3,2,8,128]{5,4,3,2,1,0:T(8,128)S(1)}, f32[2,4]{1,0:T(2,128)S(1)}, f32[8,128]{1,0:T(8,128)S(1)}, f32[...) custom-call(f32[2,3,3,2,8,128]{5,4,3,2,1,0:T(8,128)} %bitcast.22, ...), custom_call_target="tpu_custom_call" | custom-call | tf_op jit(solution)/shard_map/pallas_call | solution.py:452
  16.8 1.3 %shard_map.58 = (f32[2,3,3,2,8,128]{5,4,3,2,1,0:T(8,128)}, f32[3,2,3,3,2,8,128]{6,5,4,3,2,1,0:T(8,128)}, f32[2,4]{1,0:T(2,128)}, f32[1,1]{1,0:T(1,128)}) custom-call(f32[14,8,128]{2,1,0:T(8,128)S(1)} %get-tuple-element.14.packed_in, f32[2,3,3,2,8,128]{5,4,3,2,1,0:T(8,128)S(1)} %get-tuple-element.15.above_in, f32[2,4]{1,0:T(2,128)S(1)} %get-tuple-element.16.profile_in, ...), custom_call_target="tpu_custom_call" | custom-call | tf_op jit(solution)/shard_map/pallas_call | solution.py:484
